TPU v7x, 32 devices: a whole 2x2x4 slice. The times are simulated.
32 devices in a mesh: ctx: 2 (over y), dp: 16 (over z, x, core).
Axes of the slice: x: 2, y: 2, z: 4, core: 2. Of those that a mesh axis runs over, the one named last changes fastest.
Arguments:
- queries: bfloat16 [16, 256, 1024], P('dp', 'ctx'), may hold values from -20 to 20
- keys: bfloat16 [16, 256, 1024], P('dp', 'ctx'), may hold values from -4 to 4
- values: bfloat16 [16, 256, 1024], P('dp', 'ctx'), may hold values from -6 to 6
- d_mixed: bfloat16 [16, 256, 1024], P('dp', 'ctx'), may hold values from -6 to 6
- series_ids: int32 [16, 256], P('dp', 'ctx'), may hold values from 0 to 3, never falling along the last dimension, each value on 1 to 192 neighbouring positions
- variate_ids: int32 [16, 256], P('dp', 'ctx'), may hold values from 0 to 3
- variate_bias: float32 [2, 16], replicated, may hold values from -4 to 4
- w_out: bfloat16 [1024, 1024], P('dp'), may hold values from -0.1875 to 0.1875
Outputs:
- mixed: bfloat16 [16, 256, 1024], P('dp', 'ctx')
- q_grad: bfloat16 [16, 256, 1024], P('dp', 'ctx')
- k_grad: bfloat16 [16, 256, 1024], P('dp', 'ctx')
- v_grad: bfloat16 [16, 256, 1024], P('dp', 'ctx')
- w_grad: float32 [1024, 1024], P('dp')
- bias_grad: float32 [2, 16], replicated
Inputs may be any that keep to these rules, and one draw needn't show every extreme that they name: `series_ids`: within a packed row series numbers never fall; each series spans 1 to 192 consecutive tokens and some series spans exactly 192.
All inputs are finite; a program needn't handle non-finite values.
Results may differ from a plain program's by a relative error of at most 0.015.
Values may be sent and summed in bfloat16 or wider, within the bound.
No kernel may reach another device: no remote copies, remote signals or barrier semaphores. Data moves between devices by JAX's collectives and lax.ppermute only.
A program may use at most 128 MiB of HBM per device.

v0:
```python
import jax
import jax.numpy as jnp
from jax import lax
from jax.sharding import PartitionSpec as P

HEADS = 16
HEAD_DIM = 64
NEG = -1e30
group_width = 4


def shifted_2(shard, axis, by):
    count = lax.axis_size(axis)
    pairs = [(i, i + by) for i in range(count) if 0 <= i + by < count]
    return lax.ppermute(shard, axis, pairs)


def split_heads(block):
    rows = block.shape[0]
    return block.reshape(rows, HEADS // group_width, group_width, HEAD_DIM).transpose(1, 0, 2, 3)


def merge_heads(block):
    rows = block.shape[1]
    return block.transpose(1, 0, 2, 3).reshape(rows, HEADS * HEAD_DIM)


def stats_groups(rows_heads):
    count = rows_heads.shape[0]
    return rows_heads.reshape(count, HEADS // group_width, group_width).transpose(1, 2, 0)


def scored(q_group, k_group, bias_group, q_tag, k_tag, q_var, k_var):
    raw = jnp.einsum(
        "qhd,khd->hqk", q_group, k_group, preferred_element_type=jnp.float32
    ) * HEAD_DIM ** (-0.5)
    same = (q_var[:, None] == k_var[None, :])[None]
    allowed = (q_tag[:, None] == k_tag[None, :])[None]
    shifted = raw + jnp.where(same, bias_group[0][:, None, None], bias_group[1][:, None, None])
    return (jnp.where(allowed, shifted, NEG), allowed, same)


def joined(pieces):
    return [jnp.concatenate(items, axis=0) for items in zip(*pieces)]


def on_device(queries, keys, values, d_mixed, series_ids, variate_ids, variate_bias, w_out):
    query = queries[0]
    key_rows = keys[0]
    value_rows = values[0]
    upstream = d_mixed[0]
    tags = series_ids[0] + 1
    variety = variate_ids[0]
    tok = query.shape[0]
    n_ctx = lax.axis_size("ctx")
    most = tok * n_ctx // 2 + tok // 2
    reach = min((most - 2) // tok + 1, n_ctx - 1)
    scale = HEAD_DIM ** (-0.5)
    w_full = lax.all_gather(w_out, "dp", axis=0, tiled=True)
    d_context = lax.dot_general(
        upstream, w_full, (((1,), (1,)), ((), ())), preferred_element_type=jnp.float32
    ).astype(jnp.bfloat16)
    bias_groups = variate_bias.reshape(2, HEADS // group_width, group_width).transpose(1, 0, 2)
    pieces = [(key_rows, value_rows, tags, variety)]
    for dist in range(1, reach + 1):
        pieces.append(shifted_2((key_rows, value_rows, tags, variety), "ctx", dist))
        pieces.append(shifted_2((key_rows, value_rows, tags, variety), "ctx", -dist))
    key_set, value_set, key_tags, key_vars = joined(pieces)
    q_groups = split_heads(query)
    k_groups = split_heads(key_set)
    v_groups = split_heads(value_set)

    def forward_group(items):
        q_group, k_group, v_group, bias_group = items
        scores, allowed, same = scored(
            q_group, k_group, bias_group, tags, key_tags, variety, key_vars
        )
        top = jnp.max(scores, axis=2, keepdims=True)
        total = jnp.sum(jnp.where(allowed, jnp.exp(scores - top), 0.0), axis=2, keepdims=True)
        lse = top + jnp.log(total)
        probs = jnp.where(allowed, jnp.exp(scores - lse), 0.0)
        context = jnp.einsum(
            "hqk,khd->qhd", probs.astype(jnp.bfloat16), v_group, preferred_element_type=jnp.float32
        )
        return (context, lse[:, :, 0], probs)

    context_groups, lse_groups, prob_groups = lax.map(
        forward_group, (q_groups, k_groups, v_groups, bias_groups)
    )
    context = merge_heads(context_groups)
    context_bf = context.astype(jnp.bfloat16)
    delta_rows = jnp.sum(
        (d_context.astype(jnp.float32) * context).reshape(tok, HEADS, HEAD_DIM), axis=2
    )
    lse_rows = lse_groups.transpose(2, 0, 1).reshape(tok, HEADS)
    d_groups = split_heads(d_context)
    delta_groups = stats_groups(delta_rows)

    def query_group(items):
        k_group, v_group, d_group, probs, delta_group, bias_group = items
        same = (variety[:, None] == key_vars[None, :])[None]
        dprob = jnp.einsum("qhd,khd->hqk", d_group, v_group, preferred_element_type=jnp.float32)
        dscore = probs * (dprob - delta_group[:, :, None])
        grads = (
            jnp.einsum(
                "hqk,khd->qhd",
                dscore.astype(jnp.bfloat16),
                k_group,
                preferred_element_type=jnp.float32,
            )
            * scale
        )
        sums = jnp.stack(
            [
                jnp.sum(jnp.where(same, dscore, 0.0), axis=(1, 2)),
                jnp.sum(jnp.where(same, 0.0, dscore), axis=(1, 2)),
            ]
        )
        return (grads, sums)

    q_grads, sum_groups = lax.map(
        query_group, (k_groups, v_groups, d_groups, prob_groups, delta_groups, bias_groups)
    )
    bias_terms = sum_groups.transpose(1, 0, 2).reshape(2, HEADS)
    front = [(query, d_context, tags, variety)]
    numbers = [(lse_rows, delta_rows)]
    for dist in range(1, reach + 1):
        front.append(shifted_2((query, d_context, tags, variety), "ctx", dist))
        numbers.append(shifted_2((lse_rows, delta_rows), "ctx", dist))
        front.append(shifted_2((query, d_context, tags, variety), "ctx", -dist))
        numbers.append(shifted_2((lse_rows, delta_rows), "ctx", -dist))
    remote_q, remote_d, remote_tags, remote_vars = joined(front)
    remote_lse, remote_delta = joined(numbers)

    def key_group(items):
        q_group, d_group, lse_group, delta_group, k_group, v_group, bias_group = items
        scores, allowed, same = scored(
            q_group, k_group, bias_group, remote_tags, tags, remote_vars, variety
        )
        probs = jnp.where(allowed, jnp.exp(scores - lse_group[:, :, None]), 0.0)
        dprob = jnp.einsum("qhd,khd->hqk", d_group, v_group, preferred_element_type=jnp.float32)
        dscore = probs * (dprob - delta_group[:, :, None])
        k_grad = (
            jnp.einsum(
                "hqk,qhd->khd",
                dscore.astype(jnp.bfloat16),
                q_group,
                preferred_element_type=jnp.float32,
            )
            * scale
        )
        v_grad = jnp.einsum(
            "hqk,qhd->khd", probs.astype(jnp.bfloat16), d_group, preferred_element_type=jnp.float32
        )
        return (k_grad, v_grad)

    k_grads, v_grads = lax.map(
        key_group,
        (
            split_heads(remote_q),
            split_heads(remote_d),
            stats_groups(remote_lse),
            stats_groups(remote_delta),
            split_heads(key_rows),
            split_heads(value_rows),
            bias_groups,
        ),
    )
    q_out = merge_heads(q_grads).astype(jnp.bfloat16)
    k_out = merge_heads(k_grads).astype(jnp.bfloat16)
    v_out = merge_heads(v_grads).astype(jnp.bfloat16)
    mixed = jnp.dot(context_bf, w_full, preferred_element_type=jnp.float32).astype(jnp.bfloat16)
    partial_rows = lax.psum_scatter(
        lax.dot_general(
            context_bf, upstream, (((0,), (0,)), ((), ())), preferred_element_type=jnp.float32
        ),
        "dp",
        scatter_dimension=0,
        tiled=True,
    )
    w_grad = lax.psum(partial_rows, "ctx")
    bias_grad = lax.psum(bias_terms, ("ctx", "dp"))
    return (mixed[None], q_out[None], k_out[None], v_out[None], w_grad, bias_grad)


def solution(mesh):
    return jax.shard_map(
        on_device,
        mesh=mesh,
        in_specs=(
            P("dp", "ctx", None),
            P("dp", "ctx", None),
            P("dp", "ctx", None),
            P("dp", "ctx", None),
            P("dp", "ctx"),
            P("dp", "ctx"),
            P(),
            P("dp", None),
        ),
        out_specs=(
            P("dp", "ctx", None),
            P("dp", "ctx", None),
            P("dp", "ctx", None),
            P("dp", "ctx", None),
            P("dp", None),
            P(),
        ),
        check_vma=False,
    )
```

profile of v0, /device:TPU:0, one launch (start us, length us, event | category | flops | bytes accessed | tf_op | source)
XLA Modules:
  0.0 179.6 jit_solution(639569366921417282)
XLA Ops:
  8.4 4.9 %collective-permute-start = (bf16[128,1024]{0,1:T(8,128)(2,1)S(1)}, bf16[128,1024]{0,1:T(8,128)(2,1)S(1)}, u32[]{:S(2)}, u32[]{:S(2)}) collective-permute-start(bf16[128,1024]{0,1:T(8,128)(2,1)S(1)} %bitcast.263), channel_id=1, source_target_pairs={{0,16},{1,17},{2,18},{3,19},{4,20},{5,21},{6,22},{7,23},{8,24},{9,... | collective-permute-start | bytes 786440 | tf_op jit(solution)/shard_map/ppermute | solution.py:15
  13.4 1.3 collective-permute-start.1
  14.7 4.6 %collective-permute-start.4 = (bf16[128,1024]{1,0:T(8,128)(2,1)}, bf16[128,1024]{1,0:T(8,128)(2,1)S(1)}, u32[]{:S(2)}, u32[]{:S(2)}) collective-permute-start(bf16[128,1024]{1,0:T(8,128)(2,1)} %bitcast.278), channel_id=1, source_target_pairs={{0,16},{1,17},{2,18},{3,19},{4,20},{5,21},{6,22},{7,23},{8,24},{9,... | collective-permute-start | bytes 786440 | tf_op jit(solution)/shard_map/ppermute | solution.py:15
  21.2 1.3 collective-permute-start.3
  24.6 4.4 %collective-permute-start.6 = (s32[128]{0:T(128)}, s32[128]{0:T(128)S(1)}, u32[]{:S(2)}, u32[]{:S(2)}) collective-permute-start(s32[128]{0:T(128)} %bitcast.285), channel_id=1, source_target_pairs={{0,16},{1,17},{2,18},{3,19},{4,20},{5,21},{6,22},{7,23},{8,24},{9,... | collective-permute-start | bytes 1544 | tf_op jit(solution)/shard_map/ppermute | solution.py:15
  30.2 1.3 collective-permute-start.7
  31.5 1.3 collective-permute-start.5
  32.8 2.8 %collective-permute-done.7 = s32[128]{0:T(128)S(1)} collective-permute-done((s32[128]{0:T(128)S(1)}, s32[128]{0:T(128)S(1)}, u32[]{:S(2)}, u32[]{:S(2)}) %collective-permute-start.7) | collective-permute-done | bytes 544 | tf_op jit(solution)/shard_map/ppermute | solution.py:15
  37.8 2.0 %collective-permute-done.5 = bf16[128,1024]{1,0:T(8,128)(2,1)S(1)} collective-permute-done((bf16[128,1024]{1,0:T(8,128)(2,1)S(1)}, bf16[128,1024]{1,0:T(8,128)(2,1)S(1)}, u32[]{:S(2)}, u32[]{:S(2)}) %collective-permute-start.5) | collective-permute-done | bytes 262176 | tf_op jit(solution)/shard_map/ppermute | solution.py:15
  41.7 9.7 %while.41 = (s32[]{:T(128)}, f32[4,128,4,64]{1,3,2,0:T(8,128)S(1)}, f32[4,4,128]{2,1,0:T(4,128)S(1)}, f32[4,4,128,384]{3,2,1,0:T(8,128)}, bf16[4,384,4,64]{1,3,2...) while((s32[]{:T(128)}, f32[4,128,4,64]{1,3,2,0:T(8,128)S(1)}, ...), condition=%wide.region_3.4_spmd.clone, body=%wide.region_0.3_spmd.sunk.clone | while | flops 52985344 | bytes 4892413 | solution.py:87
  51.5 2.6 %fusion.62 = f32[1024,1024]{1,0:T(8,128)} fusion(bf16[128,1024]{0,1:T(8,128)(2,1)S(1)} %bitcast.267, bf16[1,128,1024]{2,1,0:T(8,128)(2,1)S(1)} %copy-done), kind=kOutput, calls=%fused_computation.97 | convolution fusion | flops 268435456 | bytes 4718592 | tf_op jit(solution)/shard_map/dot_general | solution.py:174
  55.1 1.5 collective-permute-start.8
  59.3 4.5 %collective-permute-start.10 = (f32[128,16]{0,1:T(8,128)S(1)}, f32[128,16]{0,1:T(8,128)S(1)}, u32[]{:S(2)}, u32[]{:S(2)}) collective-permute-start(f32[128,16]{0,1:T(8,128)S(1)} %bitcast.295), channel_id=1, source_target_pairs={{0,16},{1,17},{2,18},{3,19},{4,20},{5,21},{6,22},{7,23},{8,24},{9,... | collective-permute-start | bytes 24584 | tf_op jit(solution)/shard_map/ppermute | solution.py:15
  66.7 2.7 %collective-permute-done.11 = f32[128,16]{0,1:T(8,128)S(1)} collective-permute-done((f32[128,16]{0,1:T(8,128)S(1)}, f32[128,16]{0,1:T(8,128)S(1)}, u32[]{:S(2)}, u32[]{:S(2)}) %collective-permute-start.11) | collective-permute-done | bytes 8224 | tf_op jit(solution)/shard_map/ppermute | solution.py:15
  69.4 3.1 %convert_multiply_fusion = (f32[128,1024]{1,0:T(8,128)S(1)}, bf16[128,1024]{1,0:T(8,128)(2,1)}) fusion(f32[128,1024]{1,0:T(8,128)S(1)} %copy.39, bf16[1024,1024]{1,0:T(8,128)(2,1)} %all-gather.2.cloned.1.call-done, bf16[1,128,1024]{2,1,0:T(8,128)(2,1)S(1)} %copy-done), kind=kOutput, calls=%fused_computation.96 | convolution fusion | flops 268828672 | bytes 3670016 | tf_op jit(solution)/shard_map/dot_general | solution.py:60
  73.4 1.9 %collective-permute-start.14 = (f32[128,16]{0,1:T(8,128)}, f32[128,16]{0,1:T(8,128)S(1)}, u32[]{:S(2)}, u32[]{:S(2)}) collective-permute-start(f32[128,16]{0,1:T(8,128)} %bitcast_reduce_fusion), channel_id=1, source_target_pairs={{0,16},{1,17},{2,18},{3,19},{4,20},{5,21},{6,22},{7,23},{8,24},{9,... | collective-permute-start | bytes 24584 | tf_op jit(solution)/shard_map/ppermute | solution.py:15
  76.6 5.3 %collective-permute-start.12 = (bf16[128,1024]{1,0:T(8,128)(2,1)}, bf16[128,1024]{1,0:T(8,128)(2,1)}, u32[]{:S(2)}, u32[]{:S(2)}) collective-permute-start(bf16[128,1024]{1,0:T(8,128)(2,1)} %get-tuple-element.364), channel_id=1, source_target_pairs={{0,16},{1,17},{2,18},{3,19},{4,20},{5,21},{6,22},{7,23},{8,24},{9,... | collective-permute-start | bytes 786440 | tf_op jit(solution)/shard_map/ppermute | solution.py:15
  83.1 1.8 %copy.38 = bf16[128,1024]{0,1:T(8,128)(2,1)} copy(bf16[128,1024]{1,0:T(8,128)(2,1)} %get-tuple-element.364) | data formatting | bytes 524288 | tf_op jit(solution)/shard_map/convert_element_type | solution.py:62
  84.9 15.8 %while.42 = (s32[]{:T(128)}, bf16[4,128,4,64]{1,3,2,0:T(8,128)(2,1)S(1)}, f32[4,2,4]{2,1,0:T(2,128)S(1)}, bf16[4,384,4,64]{1,3,2,0:T(8,128)(2,1)}, f32[4,4,128,3...) while((s32[]{:T(128)}, ...), condition=%wide.region_8.9_spmd.clone, body=%wide.region_5.8_spmd.sunk.clone | while | flops 51789824 | bytes 2273933 | solution.py:121
  85.9 1.8 %select_reduce_fusion.8 = (f32[4]{0:T(128)S(1)}, f32[4]{0:T(128)S(1)}, bf16[4,128,384]{2,1,0:T(8,128)(2,1)S(1)}) fusion(pred[128,384]{1,0:T(8,128)(4,1)S(1)} %broadcast_compare_fusion.12, f32[4,128]{1,0:T(4,128)S(1)} %dynamic-slice_bitcast_fusion.7, bf16[4,384,4,64]{1,3,2,0:T(8,128)(2,1)} %get-tuple-element.778, s32[]{:T(128)} %get-tuple-element.762, ...), kind=kOutput, calls=%fused_computation.34.clone.1.clone | convolution fusion | flops 26542072 | bytes 1494560 | tf_op jit(solution)/shard_map/while/body/eval_jaxpr/qhd,khd->hqk/dot_general | solution.py:102
  89.8 1.8 %select_reduce_fusion.8 = (f32[4]{0:T(128)S(1)}, f32[4]{0:T(128)S(1)}, bf16[4,128,384]{2,1,0:T(8,128)(2,1)S(1)}) fusion(pred[128,384]{1,0:T(8,128)(4,1)S(1)} %broadcast_compare_fusion.12, f32[4,128]{1,0:T(4,128)S(1)} %dynamic-slice_bitcast_fusion.7, bf16[4,384,4,64]{1,3,2,0:T(8,128)(2,1)} %get-tuple-element.778, s32[]{:T(128)} %get-tuple-element.762, ...), kind=kOutput, calls=%fused_computation.34.clone.1.clone | convolution fusion | flops 26542072 | bytes 1494560 | tf_op jit(solution)/shard_map/while/body/eval_jaxpr/qhd,khd->hqk/dot_general | solution.py:102
  93.6 1.8 select_reduce_fusion.8
  97.4 2.0 %select_reduce_fusion.8 = (f32[4]{0:T(128)S(1)}, f32[4]{0:T(128)S(1)}, bf16[4,128,384]{2,1,0:T(8,128)(2,1)S(1)}) fusion(pred[128,384]{1,0:T(8,128)(4,1)S(1)} %broadcast_compare_fusion.12, f32[4,128]{1,0:T(4,128)S(1)} %dynamic-slice_bitcast_fusion.7, bf16[4,384,4,64]{1,3,2,0:T(8,128)(2,1)} %get-tuple-element.778, s32[]{:T(128)} %get-tuple-element.762, ...), kind=kOutput, calls=%fused_computation.34.clone.1.clone | convolution fusion | flops 26542072 | bytes 1494560 | tf_op jit(solution)/shard_map/while/body/eval_jaxpr/qhd,khd->hqk/dot_general | solution.py:102
  102.0 42.5 %psum.15 = f32[2,16]{1,0:T(2,128)} all-reduce(f32[2,16]{1,0:T(2,128)S(1)} %reshape.290), channel_id=1, replica_groups=mesh['ctx'=2,'dp'=16] {'ctx','dp'}, use_global_device_ids=true, to_apply=%region_13.14 | all-reduce | flops 32 | bytes 256 | tf_op jit(solution)/shard_map/psum | solution.py:182
  147.7 12.6 %while.43 = (s32[]{:T(128)}, bf16[4,128,4,64]{1,3,2,0:T(8,128)(2,1)S(1)}, bf16[4,128,4,64]{1,3,2,0:T(8,128)(2,1)}, bf16[4,384,4,64]{1,3,2,0:T(8,128)(2,1)S(1)}, ...) while((s32[]{:T(128)}, ...), condition=%wide.region_10.11_spmd.clone, body=%wide.region_9.10_spmd.sunk.clone | while | flops 102760448 | bytes 4109073 | solution.py:157
  148.0 1.4 fusion.120
  151.1 1.4 fusion.120
  154.2 1.4 fusion.120
  157.4 1.4 fusion.120
  161.2 1.8 copy.49
  163.0 8.4 %all-reduce.2.cloned.1.call-done = f32[64,1024]{1,0:T(8,128)} async-done(((f32[64,1024]{1,0:T(8,128)}), f32[64,1024]{1,0:T(8,128)}) %all-reduce.2.cloned.1.call-update) | async-done | bytes 262160 | tf_op jit(solution)/shard_map/psum | solution.py:181
  171.4 1.7 copy.100
  (168 shorter events, 50.4 us)
Async XLA Ops:
  7.2 44.3 %copy-start = (bf16[1,128,1024]{2,1,0:T(8,128)(2,1)S(1)}, bf16[1,128,1024]{2,1,0:T(8,128)(2,1)}, u32[]{:S(2)}) copy-start(bf16[1,128,1024]{2,1,0:T(8,128)(2,1)} %param.17) | copy-start | bytes 786436
  7.2 24.3 %copy-start.7 = (bf16[1,128,1024]{2,1,0:T(8,128)(2,1)S(1)}, bf16[1,128,1024]{2,1,0:T(8,128)(2,1)}, u32[]{:S(2)}) copy-start(bf16[1,128,1024]{2,1,0:T(8,128)(2,1)} %param.15) | copy-start | bytes 786436
  7.2 23.0 %copy-start.11 = (s32[1,128]{1,0:T(1,128)S(1)}, s32[1,128]{1,0:T(1,128)}, u32[]{:S(2)}) copy-start(s32[1,128]{1,0:T(1,128)} %param.19) | copy-start | bytes 1540
  7.2 22.9 %copy-start.12 = (f32[2,16]{1,0:T(2,128)S(1)}, f32[2,16]{1,0:T(2,128)}, u32[]{:S(2)}) copy-start(f32[2,16]{1,0:T(2,128)} %param.20) | copy-start | bytes 388
  7.2 62.2 %all-gather.2.cloned.1.call-start = ((), (), s32[]{:S(2)}) async-start(), calls=%async_computation.1 | async-start | bytes 2228224 | tf_op jit(solution)/shard_map/all_gather | solution.py:59
  8.4 27.4 %collective-permute-start = (bf16[128,1024]{0,1:T(8,128)(2,1)S(1)}, bf16[128,1024]{0,1:T(8,128)(2,1)S(1)}, u32[]{:S(2)}, u32[]{:S(2)}) collective-permute-start(bf16[128,1024]{0,1:T(8,128)(2,1)S(1)} %bitcast.263), channel_id=1, source_target_pairs={{0,16},{1,17},{2,18},{3,19},{4,20},{5,21},{6,22},{7,23},{8,24},{9,... | collective-permute-start | bytes 786440 | tf_op jit(solution)/shard_map/ppermute | solution.py:15
  13.4 22.5 %collective-permute-start.1 = (bf16[128,1024]{0,1:T(8,128)(2,1)S(1)}, bf16[128,1024]{0,1:T(8,128)(2,1)S(1)}, u32[]{:S(2)}, u32[]{:S(2)}) collective-permute-start(bf16[128,1024]{0,1:T(8,128)(2,1)S(1)} %bitcast.264), channel_id=1, source_target_pairs={{16,0},{17,1},{18,2},{19,3},{20,4},{21,5},{22,6},{23,7},{24,8},{25... | collective-permute-start | bytes 786440 | tf_op jit(solution)/shard_map/ppermute | solution.py:15
  14.7 21.0 %collective-permute-start.4 = (bf16[128,1024]{1,0:T(8,128)(2,1)}, bf16[128,1024]{1,0:T(8,128)(2,1)S(1)}, u32[]{:S(2)}, u32[]{:S(2)}) collective-permute-start(bf16[128,1024]{1,0:T(8,128)(2,1)} %bitcast.278), channel_id=1, source_target_pairs={{0,16},{1,17},{2,18},{3,19},{4,20},{5,21},{6,22},{7,23},{8,24},{9,... | collective-permute-start | bytes 786440 | tf_op jit(solution)/shard_map/ppermute | solution.py:15
  19.9 4.7 %collective-permute-start.2 = (s32[128]{0:T(128)S(1)}, s32[128]{0:T(128)S(1)}, u32[]{:S(2)}, u32[]{:S(2)}) collective-permute-start(s32[128]{0:T(128)S(1)} %add_bitcast_fusion), channel_id=1, source_target_pairs={{0,16},{1,17},{2,18},{3,19},{4,20},{5,21},{6,22},{7,23},{8,24},{9,... | collective-permute-start | bytes 1544 | tf_op jit(solution)/shard_map/ppermute | solution.py:15
  21.2 9.0 %collective-permute-start.3 = (s32[128]{0:T(128)S(1)}, s32[128]{0:T(128)S(1)}, u32[]{:S(2)}, u32[]{:S(2)}) collective-permute-start(s32[128]{0:T(128)S(1)} %add_bitcast_fusion), channel_id=1, source_target_pairs={{16,0},{17,1},{18,2},{19,3},{20,4},{21,5},{22,6},{23,7},{24,8},{25... | collective-permute-start | bytes 1544 | tf_op jit(solution)/shard_map/ppermute | solution.py:15
  22.5 125.2 %reduce-scatter.2.cloned.1.call-start = ((), (), s32[]{:S(2)}) async-start(), calls=%async_computation.2 | async-start | bytes 4456448 | tf_op jit(solution)/shard_map/reduce_scatter | solution.py:173
  23.7 17.0 %copy-start.6 = (bf16[1,128,1024]{1,2,0:T(8,128)(2,1)}, bf16[1,128,1024]{1,2,0:T(8,128)(2,1)S(1)}, u32[]{:S(2)}) copy-start(bf16[1,128,1024]{1,2,0:T(8,128)(2,1)S(1)} %copy.34) | copy-start | bytes 786436
  24.6 6.9 %collective-permute-start.6 = (s32[128]{0:T(128)}, s32[128]{0:T(128)S(1)}, u32[]{:S(2)}, u32[]{:S(2)}) collective-permute-start(s32[128]{0:T(128)} %bitcast.285), channel_id=1, source_target_pairs={{0,16},{1,17},{2,18},{3,19},{4,20},{5,21},{6,22},{7,23},{8,24},{9,... | collective-permute-start | bytes 1544 | tf_op jit(solution)/shard_map/ppermute | solution.py:15
  30.2 5.5 %collective-permute-start.7 = (s32[128]{0:T(128)S(1)}, s32[128]{0:T(128)S(1)}, u32[]{:S(2)}, u32[]{:S(2)}) collective-permute-start(s32[128]{0:T(128)S(1)} %bitcast.286), channel_id=1, source_target_pairs={{16,0},{17,1},{18,2},{19,3},{20,4},{21,5},{22,6},{23,7},{24,8},{25... | collective-permute-start | bytes 1544 | tf_op jit(solution)/shard_map/ppermute | solution.py:15
  31.5 8.3 %collective-permute-start.5 = (bf16[128,1024]{1,0:T(8,128)(2,1)S(1)}, bf16[128,1024]{1,0:T(8,128)(2,1)S(1)}, u32[]{:S(2)}, u32[]{:S(2)}) collective-permute-start(bf16[128,1024]{1,0:T(8,128)(2,1)S(1)} %bitcast.279), channel_id=1, source_target_pairs={{16,0},{17,1},{18,2},{19,3},{20,4},{21,5},{22,6},{23,7},{24,8},{25... | collective-permute-start | bytes 786440 | tf_op jit(solution)/shard_map/ppermute | solution.py:15
  35.9 0.7 copy-start.9
  35.9 0.8 copy-start.10
  51.4 2.7 %copy-start.3 = (bf16[4,384,4,64]{1,3,2,0:T(8,128)(2,1)}, bf16[4,384,4,64]{1,3,2,0:T(8,128)(2,1)S(1)}, u32[]{:S(2)}) copy-start(bf16[4,384,4,64]{1,3,2,0:T(8,128)(2,1)S(1)} %get-tuple-element.836) | copy-start | bytes 2359300
  51.4 2.7 %copy-start.4 = (bf16[4,384,4,64]{1,3,2,0:T(8,128)(2,1)}, bf16[4,384,4,64]{1,3,2,0:T(8,128)(2,1)S(1)}, u32[]{:S(2)}) copy-start(bf16[4,384,4,64]{1,3,2,0:T(8,128)(2,1)S(1)} %get-tuple-element.837) | copy-start | bytes 2359300
  54.1 1.0 copy-start.8
  54.1 117.2 %all-reduce.2.cloned.1.call-start = ((), (), s32[]{:S(2)}) async-start(), calls=%async_computation.3 | async-start | bytes 524288 | tf_op jit(solution)/shard_map/psum | solution.py:181
  55.1 10.1 %collective-permute-start.8 = (bf16[128,1024]{1,0:T(8,128)(2,1)S(1)}, bf16[128,1024]{1,0:T(8,128)(2,1)S(1)}, u32[]{:S(2)}, u32[]{:S(2)}) collective-permute-start(bf16[128,1024]{1,0:T(8,128)(2,1)S(1)} %bitcast.280), channel_id=1, source_target_pairs={{0,16},{1,17},{2,18},{3,19},{4,20},{5,21},{6,22},{7,23},{8,24},{9,... | collective-permute-start | bytes 786440 | tf_op jit(solution)/shard_map/ppermute | solution.py:15
  56.5 8.8 %collective-permute-start.9 = (bf16[128,1024]{1,0:T(8,128)(2,1)S(1)}, bf16[128,1024]{1,0:T(8,128)(2,1)S(1)}, u32[]{:S(2)}, u32[]{:S(2)}) collective-permute-start(bf16[128,1024]{1,0:T(8,128)(2,1)S(1)} %bitcast.281), channel_id=1, source_target_pairs={{16,0},{17,1},{18,2},{19,3},{20,4},{21,5},{22,6},{23,7},{24,8},{25... | collective-permute-start | bytes 786440 | tf_op jit(solution)/shard_map/ppermute | solution.py:15
  59.3 7.4 %collective-permute-start.10 = (f32[128,16]{0,1:T(8,128)S(1)}, f32[128,16]{0,1:T(8,128)S(1)}, u32[]{:S(2)}, u32[]{:S(2)}) collective-permute-start(f32[128,16]{0,1:T(8,128)S(1)} %bitcast.295), channel_id=1, source_target_pairs={{0,16},{1,17},{2,18},{3,19},{4,20},{5,21},{6,22},{7,23},{8,24},{9,... | collective-permute-start | bytes 24584 | tf_op jit(solution)/shard_map/ppermute | solution.py:15
  63.8 5.5 %collective-permute-start.11 = (f32[128,16]{0,1:T(8,128)S(1)}, f32[128,16]{0,1:T(8,128)S(1)}, u32[]{:S(2)}, u32[]{:S(2)}) collective-permute-start(f32[128,16]{0,1:T(8,128)S(1)} %bitcast.296), channel_id=1, source_target_pairs={{16,0},{17,1},{18,2},{19,3},{20,4},{21,5},{22,6},{23,7},{24,8},{25... | collective-permute-start | bytes 24584 | tf_op jit(solution)/shard_map/ppermute | solution.py:15
  73.4 71.9 %collective-permute-start.14 = (f32[128,16]{0,1:T(8,128)}, f32[128,16]{0,1:T(8,128)S(1)}, u32[]{:S(2)}, u32[]{:S(2)}) collective-permute-start(f32[128,16]{0,1:T(8,128)} %bitcast_reduce_fusion), channel_id=1, source_target_pairs={{0,16},{1,17},{2,18},{3,19},{4,20},{5,21},{6,22},{7,23},{8,24},{9,... | collective-permute-start | bytes 24584 | tf_op jit(solution)/shard_map/ppermute | solution.py:15
  75.3 70.0 %collective-permute-start.15 = (f32[128,16]{0,1:T(8,128)}, f32[128,16]{0,1:T(8,128)S(1)}, u32[]{:S(2)}, u32[]{:S(2)}) collective-permute-start(f32[128,16]{0,1:T(8,128)} %bitcast_reduce_fusion), channel_id=1, source_target_pairs={{16,0},{17,1},{18,2},{19,3},{20,4},{21,5},{22,6},{23,7},{24,8},{25... | collective-permute-start | bytes 24584 | tf_op jit(solution)/shard_map/ppermute | solution.py:15
  76.6 69.5 %collective-permute-start.12 = (bf16[128,1024]{1,0:T(8,128)(2,1)}, bf16[128,1024]{1,0:T(8,128)(2,1)}, u32[]{:S(2)}, u32[]{:S(2)}) collective-permute-start(bf16[128,1024]{1,0:T(8,128)(2,1)} %get-tuple-element.364), channel_id=1, source_target_pairs={{0,16},{1,17},{2,18},{3,19},{4,20},{5,21},{6,22},{7,23},{8,24},{9,... | collective-permute-start | bytes 786440 | tf_op jit(solution)/shard_map/ppermute | solution.py:15
  81.8 64.2 %collective-permute-start.13 = (bf16[128,1024]{1,0:T(8,128)(2,1)}, bf16[128,1024]{1,0:T(8,128)(2,1)}, u32[]{:S(2)}, u32[]{:S(2)}) collective-permute-start(bf16[128,1024]{1,0:T(8,128)(2,1)} %get-tuple-element.364), channel_id=1, source_target_pairs={{16,0},{17,1},{18,2},{19,3},{20,4},{21,5},{22,6},{23,7},{24,8},{25... | collective-permute-start | bytes 786440 | tf_op jit(solution)/shard_map/ppermute | solution.py:15
  84.9 15.9 %copy-start.1 = (bf16[1024,1024]{1,0:T(8,128)(2,1)S(1)}, bf16[1024,1024]{1,0:T(8,128)(2,1)}, u32[]{:S(2)}) copy-start(bf16[1024,1024]{1,0:T(8,128)(2,1)} %all-gather.2.cloned.1.call-done) | copy-start | bytes 6291460
  146.0 1.7 copy-start.2
  146.0 1.7 copy-start.5
Sparse Core Ops, SparseCore 0:
  22.6 43.8 all-gather.1
  70.4 72.1 reduce-scatter.1
  147.8 23.4 all-reduce.1
where the time goes:
time: 181 us; the launch traced here: 180 us
  blocking collectives  42.5 us (23%)
  starting transfers between devices  38.7 us (21%)
  matrix products  33.7 us (19%)
  local copies, waits for them, and re-layouts  19.3 us (11%)
  waiting for transfers between devices  16.9 us (9%)
  between operations  14.2 us (8%)
  other arithmetic  13.7 us (8%)
    psum x1, blocking collectives, on_device(): bias_grad = lax.psum(bias_terms, ('ctx', 'dp'))  42.5 us
    ppermute x16, starting transfers between devices, shifted_2(): return lax.ppermute(shard, axis, pairs)  38.6 us
    unnamed x35, local copies, waits for them, and re-layouts  11.7 us
    psum x1, waiting for transfers between devices, on_device(): w_grad = lax.psum(partial_rows, 'ctx')  8.41 us
    ppermute x16, waiting for transfers between devices, shifted_2(): return lax.ppermute(shard, axis, pairs)  8.41 us
    dot_general x4, matrix products, query_group(): jnp.einsum('qhd,khd->hqk', d_group, v_group, preferred_element_type=jnp.f...  7.44 us
    dot_general x8, matrix products, scored(): jnp.einsum('qhd,khd->hqk', q_group, k_group, preferred_element_type=jnp.f...  7.35 us
    dot_general x4, matrix products, query_group(): jnp.einsum('hqk,khd->qhd', dscore.astype(jnp.bfloat16), k_group, preferre...  4.94 us
  transfers between devices with their start and end apart: 19, of which 5 were waited for; matrix products, arithmetic and copies ran while one was open for 35% of the time, Pallas kernels for 0%

commit v1 on v0

--- a/solution.py
+++ b/solution.py
@@ -1,3 +1,4 @@
+import functools
 import jax
 import jax.numpy as jnp
 from jax import lax
@@ -7,6 +8,14 @@
 HEAD_DIM = 64
 NEG = -1e30
 group_width = 4
+
+
+def press_the_heaps(piece_in, peer_axis):
+    y1 = lax.all_gather(piece_in, peer_axis)
+    return jnp.sum(y1, axis=0)
+
+
+change_ports_by_axis = functools.partial(press_the_heaps, peer_axis=("ctx", "dp"))
 
 
 def shifted_2(shard, axis, by):
@@ -179,7 +188,7 @@
         tiled=True,
     )
     w_grad = lax.psum(partial_rows, "ctx")
-    bias_grad = lax.psum(bias_terms, ("ctx", "dp"))
+    bias_grad = change_ports_by_axis(bias_terms)
     return (mixed[None], q_out[None], k_out[None], v_out[None], w_grad, bias_grad)
 
 

time: 181 us -> 179 us (0.989)
  waiting for transfers between devices: 16.9 us -> 13.4 us
    all_gather x0 -> x1, blocking collectives: none -> 43.7 us  [press_the_heaps(): y1 = lax.all_gather(piece_in, peer_axis)]
    psum x1 -> x0, blocking collectives: 42.5 us -> none  [on_device(): bias_grad = lax.psum(bias_terms, ('ctx', 'dp'))]
    psum x1, waiting for transfers between devices: 8.41 us -> 4.89 us  [on_device(): w_grad = lax.psum(partial_rows, 'ctx')]
where the time goes in v1:
time: 179 us; the launch traced here: 177 us
  blocking collectives  43.7 us (24%)
  starting transfers between devices  38.7 us (22%)
  matrix products  33.7 us (19%)
  local copies, waits for them, and re-layouts  18.7 us (10%)
  other arithmetic  14.4 us (8%)
  between operations  14.2 us (8%)
  waiting for transfers between devices  13.4 us (7%)
    all_gather x1, blocking collectives, press_the_heaps(): y1 = lax.all_gather(piece_in, peer_axis)  43.7 us
    ppermute x16, starting transfers between devices, shifted_2(): return lax.ppermute(shard, axis, pairs)  38.6 us
    unnamed x35, local copies, waits for them, and re-layouts  11.7 us
    ppermute x16, waiting for transfers between devices, shifted_2(): return lax.ppermute(shard, axis, pairs)  8.41 us
    dot_general x4, matrix products, query_group(): jnp.einsum('qhd,khd->hqk', d_group, v_group, preferred_element_type=jnp.f...  7.44 us
    dot_general x8, matrix products, scored(): jnp.einsum('qhd,khd->hqk', q_group, k_group, preferred_element_type=jnp.f...  7.36 us
    dot_general x4, matrix products, query_group(): jnp.einsum('hqk,khd->qhd', dscore.astype(jnp.bfloat16), k_group, preferre...  4.94 us
    psum x1, waiting for transfers between devices, on_device(): w_grad = lax.psum(partial_rows, 'ctx')  4.89 us
  transfers between devices with their start and end apart: 19, of which 5 were waited for; matrix products, arithmetic and copies ran while one was open for 35% of the time, Pallas kernels for 0%

profile of v1, /device:TPU:0, one launch (start us, length us, event | category | flops | bytes accessed | tf_op | source)
XLA Modules:
  0.0 177.3 jit_solution(12168976539316292407)
XLA Ops:
  8.4 4.9 %collective-permute-start = (bf16[128,1024]{0,1:T(8,128)(2,1)S(1)}, bf16[128,1024]{0,1:T(8,128)(2,1)S(1)}, u32[]{:S(2)}, u32[]{:S(2)}) collective-permute-start(bf16[128,1024]{0,1:T(8,128)(2,1)S(1)} %bitcast.265), channel_id=1, source_target_pairs={{0,16},{1,17},{2,18},{3,19},{4,20},{5,21},{6,22},{7,23},{8,24},{9,... | collective-permute-start | bytes 786440 | tf_op jit(solution)/shard_map/ppermute | solution.py:24
  13.4 1.3 collective-permute-start.1
  14.7 4.6 %collective-permute-start.4 = (bf16[128,1024]{1,0:T(8,128)(2,1)}, bf16[128,1024]{1,0:T(8,128)(2,1)S(1)}, u32[]{:S(2)}, u32[]{:S(2)}) collective-permute-start(bf16[128,1024]{1,0:T(8,128)(2,1)} %bitcast.279), channel_id=1, source_target_pairs={{0,16},{1,17},{2,18},{3,19},{4,20},{5,21},{6,22},{7,23},{8,24},{9,... | collective-permute-start | bytes 786440 | tf_op jit(solution)/shard_map/ppermute | solution.py:24
  21.2 1.3 collective-permute-start.3
  24.6 4.4 %collective-permute-start.6 = (s32[128]{0:T(128)}, s32[128]{0:T(128)S(1)}, u32[]{:S(2)}, u32[]{:S(2)}) collective-permute-start(s32[128]{0:T(128)} %bitcast.286), channel_id=1, source_target_pairs={{0,16},{1,17},{2,18},{3,19},{4,20},{5,21},{6,22},{7,23},{8,24},{9,... | collective-permute-start | bytes 1544 | tf_op jit(solution)/shard_map/ppermute | solution.py:24
  30.2 1.3 collective-permute-start.7
  31.5 1.3 collective-permute-start.5
  32.8 2.8 %collective-permute-done.7 = s32[128]{0:T(128)S(1)} collective-permute-done((s32[128]{0:T(128)S(1)}, s32[128]{0:T(128)S(1)}, u32[]{:S(2)}, u32[]{:S(2)}) %collective-permute-start.7) | collective-permute-done | bytes 544 | tf_op jit(solution)/shard_map/ppermute | solution.py:24
  37.8 2.0 %collective-permute-done.5 = bf16[128,1024]{1,0:T(8,128)(2,1)S(1)} collective-permute-done((bf16[128,1024]{1,0:T(8,128)(2,1)S(1)}, bf16[128,1024]{1,0:T(8,128)(2,1)S(1)}, u32[]{:S(2)}, u32[]{:S(2)}) %collective-permute-start.5) | collective-permute-done | bytes 262176 | tf_op jit(solution)/shard_map/ppermute | solution.py:24
  41.7 9.7 %while.41 = (s32[]{:T(128)}, f32[4,128,4,64]{1,3,2,0:T(8,128)S(1)}, f32[4,4,128]{2,1,0:T(4,128)S(1)}, f32[4,4,128,384]{3,2,1,0:T(8,128)}, bf16[4,384,4,64]{1,3,2...) while((s32[]{:T(128)}, f32[4,128,4,64]{1,3,2,0:T(8,128)S(1)}, ...), condition=%wide.region_3.4_spmd.clone, body=%wide.region_0.3_spmd.sunk.clone | while | flops 52985344 | bytes 4892413 | solution.py:96
  51.5 2.6 %fusion.64 = f32[1024,1024]{1,0:T(8,128)} fusion(bf16[128,1024]{0,1:T(8,128)(2,1)S(1)} %bitcast.269, bf16[1,128,1024]{2,1,0:T(8,128)(2,1)S(1)} %copy-done), kind=kOutput, calls=%fused_computation.97 | convolution fusion | flops 268435456 | bytes 4718592 | tf_op jit(solution)/shard_map/dot_general | solution.py:183
  55.1 1.5 collective-permute-start.8
  59.3 4.5 %collective-permute-start.10 = (f32[128,16]{0,1:T(8,128)S(1)}, f32[128,16]{0,1:T(8,128)S(1)}, u32[]{:S(2)}, u32[]{:S(2)}) collective-permute-start(f32[128,16]{0,1:T(8,128)S(1)} %bitcast.296), channel_id=1, source_target_pairs={{0,16},{1,17},{2,18},{3,19},{4,20},{5,21},{6,22},{7,23},{8,24},{9,... | collective-permute-start | bytes 24584 | tf_op jit(solution)/shard_map/ppermute | solution.py:24
  66.7 2.7 %collective-permute-done.11 = f32[128,16]{0,1:T(8,128)S(1)} collective-permute-done((f32[128,16]{0,1:T(8,128)S(1)}, f32[128,16]{0,1:T(8,128)S(1)}, u32[]{:S(2)}, u32[]{:S(2)}) %collective-permute-start.11) | collective-permute-done | bytes 8224 | tf_op jit(solution)/shard_map/ppermute | solution.py:24
  69.4 3.1 %convert_multiply_fusion = (f32[128,1024]{1,0:T(8,128)S(1)}, bf16[128,1024]{1,0:T(8,128)(2,1)}) fusion(f32[128,1024]{1,0:T(8,128)S(1)} %copy.58, bf16[1024,1024]{1,0:T(8,128)(2,1)} %all-gather.2.cloned.1.call-done, bf16[1,128,1024]{2,1,0:T(8,128)(2,1)S(1)} %copy-done), kind=kOutput, calls=%fused_computation.96 | convolution fusion | flops 268828672 | bytes 3670016 | tf_op jit(solution)/shard_map/dot_general | solution.py:69
  73.4 1.9 %collective-permute-start.14 = (f32[128,16]{0,1:T(8,128)}, f32[128,16]{0,1:T(8,128)S(1)}, u32[]{:S(2)}, u32[]{:S(2)}) collective-permute-start(f32[128,16]{0,1:T(8,128)} %bitcast_reduce_fusion), channel_id=1, source_target_pairs={{0,16},{1,17},{2,18},{3,19},{4,20},{5,21},{6,22},{7,23},{8,24},{9,... | collective-permute-start | bytes 24584 | tf_op jit(solution)/shard_map/ppermute | solution.py:24
  76.6 5.3 %collective-permute-start.12 = (bf16[128,1024]{1,0:T(8,128)(2,1)}, bf16[128,1024]{1,0:T(8,128)(2,1)}, u32[]{:S(2)}, u32[]{:S(2)}) collective-permute-start(bf16[128,1024]{1,0:T(8,128)(2,1)} %get-tuple-element.396), channel_id=1, source_target_pairs={{0,16},{1,17},{2,18},{3,19},{4,20},{5,21},{6,22},{7,23},{8,24},{9,... | collective-permute-start | bytes 786440 | tf_op jit(solution)/shard_map/ppermute | solution.py:24
  83.1 1.8 %copy.57 = bf16[128,1024]{0,1:T(8,128)(2,1)} copy(bf16[128,1024]{1,0:T(8,128)(2,1)} %get-tuple-element.396) | data formatting | bytes 524288 | tf_op jit(solution)/shard_map/convert_element_type | solution.py:71
  84.9 15.8 %while.42 = (s32[]{:T(128)}, bf16[4,128,4,64]{1,3,2,0:T(8,128)(2,1)S(1)}, f32[4,2,4]{2,1,0:T(2,128)S(1)}, bf16[4,384,4,64]{1,3,2,0:T(8,128)(2,1)}, f32[4,4,128,3...) while((s32[]{:T(128)}, ...), condition=%wide.region_8.9_spmd.clone, body=%wide.region_5.8_spmd.sunk.clone | while | flops 51789824 | bytes 2273933 | solution.py:130
  85.9 1.8 %select_reduce_fusion.8 = (f32[4]{0:T(128)S(1)}, f32[4]{0:T(128)S(1)}, bf16[4,128,384]{2,1,0:T(8,128)(2,1)S(1)}) fusion(pred[128,384]{1,0:T(8,128)(4,1)S(1)} %broadcast_compare_fusion.12, f32[4,128]{1,0:T(4,128)S(1)} %dynamic-slice_bitcast_fusion.7, bf16[4,384,4,64]{1,3,2,0:T(8,128)(2,1)} %get-tuple-element.810, s32[]{:T(128)} %get-tuple-element.794, ...), kind=kOutput, calls=%fused_computation.34.clone.1.clone | convolution fusion | flops 26542072 | bytes 1494560 | tf_op jit(solution)/shard_map/while/body/eval_jaxpr/qhd,khd->hqk/dot_general | solution.py:111
  89.8 1.8 %select_reduce_fusion.8 = (f32[4]{0:T(128)S(1)}, f32[4]{0:T(128)S(1)}, bf16[4,128,384]{2,1,0:T(8,128)(2,1)S(1)}) fusion(pred[128,384]{1,0:T(8,128)(4,1)S(1)} %broadcast_compare_fusion.12, f32[4,128]{1,0:T(4,128)S(1)} %dynamic-slice_bitcast_fusion.7, bf16[4,384,4,64]{1,3,2,0:T(8,128)(2,1)} %get-tuple-element.810, s32[]{:T(128)} %get-tuple-element.794, ...), kind=kOutput, calls=%fused_computation.34.clone.1.clone | convolution fusion | flops 26542072 | bytes 1494560 | tf_op jit(solution)/shard_map/while/body/eval_jaxpr/qhd,khd->hqk/dot_general | solution.py:111
  93.6 1.8 %select_reduce_fusion.8 = (f32[4]{0:T(128)S(1)}, f32[4]{0:T(128)S(1)}, bf16[4,128,384]{2,1,0:T(8,128)(2,1)S(1)}) fusion(pred[128,384]{1,0:T(8,128)(4,1)S(1)} %broadcast_compare_fusion.12, f32[4,128]{1,0:T(4,128)S(1)} %dynamic-slice_bitcast_fusion.7, bf16[4,384,4,64]{1,3,2,0:T(8,128)(2,1)} %get-tuple-element.810, s32[]{:T(128)} %get-tuple-element.794, ...), kind=kOutput, calls=%fused_computation.34.clone.1.clone | convolution fusion | flops 26542072 | bytes 1494560 | tf_op jit(solution)/shard_map/while/body/eval_jaxpr/qhd,khd->hqk/dot_general | solution.py:111
  97.4 2.0 %select_reduce_fusion.8 = (f32[4]{0:T(128)S(1)}, f32[4]{0:T(128)S(1)}, bf16[4,128,384]{2,1,0:T(8,128)(2,1)S(1)}) fusion(pred[128,384]{1,0:T(8,128)(4,1)S(1)} %broadcast_compare_fusion.12, f32[4,128]{1,0:T(4,128)S(1)} %dynamic-slice_bitcast_fusion.7, bf16[4,384,4,64]{1,3,2,0:T(8,128)(2,1)} %get-tuple-element.810, s32[]{:T(128)} %get-tuple-element.794, ...), kind=kOutput, calls=%fused_computation.34.clone.1.clone | convolution fusion | flops 26542072 | bytes 1494560 | tf_op jit(solution)/shard_map/while/body/eval_jaxpr/qhd,khd->hqk/dot_general | solution.py:111
  102.8 43.7 %all_gather.7 = f32[32,2,16]{2,1,0:T(2,128)S(1)} all-gather(f32[1,2,16]{2,1,0:T(2,128)S(1)} %all_gather_reshape.3), channel_id=1, replica_groups=mesh['ctx'=2,'dp'=16] {'ctx','dp'}, dimensions={0}, use_global_device_ids=true | all-gather | bytes 4224 | tf_op jit(solution)/shard_map/all_gather | solution.py:14
  149.6 12.0 %while.43 = (s32[]{:T(128)}, bf16[4,128,4,64]{1,3,2,0:T(8,128)(2,1)S(1)}, bf16[4,128,4,64]{1,3,2,0:T(8,128)(2,1)}, bf16[4,384,4,64]{1,3,2,0:T(8,128)(2,1)S(1)}, ...) while((s32[]{:T(128)}, ...), condition=%wide.region_10.11_spmd.clone, body=%wide.region_9.10_spmd.sunk.clone | while | flops 102760448 | bytes 3781901 | solution.py:166
  149.8 1.4 fusion.122
  152.8 1.4 fusion.122
  155.8 1.4 fusion.122
  158.8 1.4 fusion.122
  162.4 1.8 %copy.67 = bf16[1,128,1024]{2,1,0:T(8,128)(2,1)} copy(bf16[1,128,1024]{1,2,0:T(8,128)(2,1)} %bitcast.79) | data formatting | bytes 524288
  164.2 4.9 %all-reduce.2.cloned.1.call-done = f32[64,1024]{1,0:T(8,128)} async-done(((f32[64,1024]{1,0:T(8,128)}), f32[64,1024]{1,0:T(8,128)}) %all-reduce.2.cloned.1.call-update) | async-done | bytes 262160 | tf_op jit(solution)/shard_map/psum | solution.py:190
  169.1 1.7 copy.107
  (161 shorter events, 50.4 us)
Async XLA Ops:
  7.2 44.3 %copy-start = (bf16[1,128,1024]{2,1,0:T(8,128)(2,1)S(1)}, bf16[1,128,1024]{2,1,0:T(8,128)(2,1)}, u32[]{:S(2)}) copy-start(bf16[1,128,1024]{2,1,0:T(8,128)(2,1)} %param.17) | copy-start | bytes 786436
  7.2 24.3 %copy-start.7 = (bf16[1,128,1024]{2,1,0:T(8,128)(2,1)S(1)}, bf16[1,128,1024]{2,1,0:T(8,128)(2,1)}, u32[]{:S(2)}) copy-start(bf16[1,128,1024]{2,1,0:T(8,128)(2,1)} %param.15) | copy-start | bytes 786436
  7.2 23.0 %copy-start.11 = (s32[1,128]{1,0:T(1,128)S(1)}, s32[1,128]{1,0:T(1,128)}, u32[]{:S(2)}) copy-start(s32[1,128]{1,0:T(1,128)} %param.19) | copy-start | bytes 1540
  7.2 22.9 %copy-start.12 = (f32[2,16]{1,0:T(2,128)S(1)}, f32[2,16]{1,0:T(2,128)}, u32[]{:S(2)}) copy-start(f32[2,16]{1,0:T(2,128)} %param.20) | copy-start | bytes 388
  7.2 62.2 %all-gather.2.cloned.1.call-start = ((), (), s32[]{:S(2)}) async-start(), calls=%async_computation.1 | async-start | bytes 2228224 | tf_op jit(solution)/shard_map/all_gather | solution.py:68
  8.4 27.4 %collective-permute-start = (bf16[128,1024]{0,1:T(8,128)(2,1)S(1)}, bf16[128,1024]{0,1:T(8,128)(2,1)S(1)}, u32[]{:S(2)}, u32[]{:S(2)}) collective-permute-start(bf16[128,1024]{0,1:T(8,128)(2,1)S(1)} %bitcast.265), channel_id=1, source_target_pairs={{0,16},{1,17},{2,18},{3,19},{4,20},{5,21},{6,22},{7,23},{8,24},{9,... | collective-permute-start | bytes 786440 | tf_op jit(solution)/shard_map/ppermute | solution.py:24
  13.4 22.5 %collective-permute-start.1 = (bf16[128,1024]{0,1:T(8,128)(2,1)S(1)}, bf16[128,1024]{0,1:T(8,128)(2,1)S(1)}, u32[]{:S(2)}, u32[]{:S(2)}) collective-permute-start(bf16[128,1024]{0,1:T(8,128)(2,1)S(1)} %bitcast.266), channel_id=1, source_target_pairs={{16,0},{17,1},{18,2},{19,3},{20,4},{21,5},{22,6},{23,7},{24,8},{25... | collective-permute-start | bytes 786440 | tf_op jit(solution)/shard_map/ppermute | solution.py:24
  14.7 21.0 %collective-permute-start.4 = (bf16[128,1024]{1,0:T(8,128)(2,1)}, bf16[128,1024]{1,0:T(8,128)(2,1)S(1)}, u32[]{:S(2)}, u32[]{:S(2)}) collective-permute-start(bf16[128,1024]{1,0:T(8,128)(2,1)} %bitcast.279), channel_id=1, source_target_pairs={{0,16},{1,17},{2,18},{3,19},{4,20},{5,21},{6,22},{7,23},{8,24},{9,... | collective-permute-start | bytes 786440 | tf_op jit(solution)/shard_map/ppermute | solution.py:24
  19.9 4.7 %collective-permute-start.2 = (s32[128]{0:T(128)S(1)}, s32[128]{0:T(128)S(1)}, u32[]{:S(2)}, u32[]{:S(2)}) collective-permute-start(s32[128]{0:T(128)S(1)} %add_bitcast_fusion), channel_id=1, source_target_pairs={{0,16},{1,17},{2,18},{3,19},{4,20},{5,21},{6,22},{7,23},{8,24},{9,... | collective-permute-start | bytes 1544 | tf_op jit(solution)/shard_map/ppermute | solution.py:24
  21.2 9.0 %collective-permute-start.3 = (s32[128]{0:T(128)S(1)}, s32[128]{0:T(128)S(1)}, u32[]{:S(2)}, u32[]{:S(2)}) collective-permute-start(s32[128]{0:T(128)S(1)} %add_bitcast_fusion), channel_id=1, source_target_pairs={{16,0},{17,1},{18,2},{19,3},{20,4},{21,5},{22,6},{23,7},{24,8},{25... | collective-permute-start | bytes 1544 | tf_op jit(solution)/shard_map/ppermute | solution.py:24
  22.5 127.0 %reduce-scatter.2.cloned.1.call-start = ((), (), s32[]{:S(2)}) async-start(), calls=%async_computation.2 | async-start | bytes 4456448 | tf_op jit(solution)/shard_map/reduce_scatter | solution.py:182
  23.7 17.0 %copy-start.6 = (bf16[1,128,1024]{1,2,0:T(8,128)(2,1)}, bf16[1,128,1024]{1,2,0:T(8,128)(2,1)S(1)}, u32[]{:S(2)}) copy-start(bf16[1,128,1024]{1,2,0:T(8,128)(2,1)S(1)} %copy.53) | copy-start | bytes 786436
  24.6 6.9 %collective-permute-start.6 = (s32[128]{0:T(128)}, s32[128]{0:T(128)S(1)}, u32[]{:S(2)}, u32[]{:S(2)}) collective-permute-start(s32[128]{0:T(128)} %bitcast.286), channel_id=1, source_target_pairs={{0,16},{1,17},{2,18},{3,19},{4,20},{5,21},{6,22},{7,23},{8,24},{9,... | collective-permute-start | bytes 1544 | tf_op jit(solution)/shard_map/ppermute | solution.py:24
  30.2 5.5 %collective-permute-start.7 = (s32[128]{0:T(128)S(1)}, s32[128]{0:T(128)S(1)}, u32[]{:S(2)}, u32[]{:S(2)}) collective-permute-start(s32[128]{0:T(128)S(1)} %bitcast.287), channel_id=1, source_target_pairs={{16,0},{17,1},{18,2},{19,3},{20,4},{21,5},{22,6},{23,7},{24,8},{25... | collective-permute-start | bytes 1544 | tf_op jit(solution)/shard_map/ppermute | solution.py:24
  31.5 8.3 %collective-permute-start.5 = (bf16[128,1024]{1,0:T(8,128)(2,1)S(1)}, bf16[128,1024]{1,0:T(8,128)(2,1)S(1)}, u32[]{:S(2)}, u32[]{:S(2)}) collective-permute-start(bf16[128,1024]{1,0:T(8,128)(2,1)S(1)} %bitcast.280), channel_id=1, source_target_pairs={{16,0},{17,1},{18,2},{19,3},{20,4},{21,5},{22,6},{23,7},{24,8},{25... | collective-permute-start | bytes 786440 | tf_op jit(solution)/shard_map/ppermute | solution.py:24
  35.9 0.7 copy-start.9
  35.9 0.8 copy-start.10
  51.4 2.7 %copy-start.2 = (bf16[4,384,4,64]{1,3,2,0:T(8,128)(2,1)}, bf16[4,384,4,64]{1,3,2,0:T(8,128)(2,1)S(1)}, u32[]{:S(2)}) copy-start(bf16[4,384,4,64]{1,3,2,0:T(8,128)(2,1)S(1)} %get-tuple-element.868) | copy-start | bytes 2359300
  51.4 2.7 %copy-start.3 = (bf16[4,384,4,64]{1,3,2,0:T(8,128)(2,1)}, bf16[4,384,4,64]{1,3,2,0:T(8,128)(2,1)S(1)}, u32[]{:S(2)}) copy-start(bf16[4,384,4,64]{1,3,2,0:T(8,128)(2,1)S(1)} %get-tuple-element.869) | copy-start | bytes 2359300
  54.1 1.0 copy-start.8
  54.1 115.0 %all-reduce.2.cloned.1.call-start = ((), (), s32[]{:S(2)}) async-start(), calls=%async_computation.3 | async-start | bytes 524288 | tf_op jit(solution)/shard_map/psum | solution.py:190
  55.1 10.1 %collective-permute-start.8 = (bf16[128,1024]{1,0:T(8,128)(2,1)S(1)}, bf16[128,1024]{1,0:T(8,128)(2,1)S(1)}, u32[]{:S(2)}, u32[]{:S(2)}) collective-permute-start(bf16[128,1024]{1,0:T(8,128)(2,1)S(1)} %bitcast.281), channel_id=1, source_target_pairs={{0,16},{1,17},{2,18},{3,19},{4,20},{5,21},{6,22},{7,23},{8,24},{9,... | collective-permute-start | bytes 786440 | tf_op jit(solution)/shard_map/ppermute | solution.py:24
  56.5 8.8 %collective-permute-start.9 = (bf16[128,1024]{1,0:T(8,128)(2,1)S(1)}, bf16[128,1024]{1,0:T(8,128)(2,1)S(1)}, u32[]{:S(2)}, u32[]{:S(2)}) collective-permute-start(bf16[128,1024]{1,0:T(8,128)(2,1)S(1)} %bitcast.282), channel_id=1, source_target_pairs={{16,0},{17,1},{18,2},{19,3},{20,4},{21,5},{22,6},{23,7},{24,8},{25... | collective-permute-start | bytes 786440 | tf_op jit(solution)/shard_map/ppermute | solution.py:24
  59.3 7.4 %collective-permute-start.10 = (f32[128,16]{0,1:T(8,128)S(1)}, f32[128,16]{0,1:T(8,128)S(1)}, u32[]{:S(2)}, u32[]{:S(2)}) collective-permute-start(f32[128,16]{0,1:T(8,128)S(1)} %bitcast.296), channel_id=1, source_target_pairs={{0,16},{1,17},{2,18},{3,19},{4,20},{5,21},{6,22},{7,23},{8,24},{9,... | collective-permute-start | bytes 24584 | tf_op jit(solution)/shard_map/ppermute | solution.py:24
  63.8 5.5 %collective-permute-start.11 = (f32[128,16]{0,1:T(8,128)S(1)}, f32[128,16]{0,1:T(8,128)S(1)}, u32[]{:S(2)}, u32[]{:S(2)}) collective-permute-start(f32[128,16]{0,1:T(8,128)S(1)} %bitcast.297), channel_id=1, source_target_pairs={{16,0},{17,1},{18,2},{19,3},{20,4},{21,5},{22,6},{23,7},{24,8},{25... | collective-permute-start | bytes 24584 | tf_op jit(solution)/shard_map/ppermute | solution.py:24
  73.4 73.8 %collective-permute-start.14 = (f32[128,16]{0,1:T(8,128)}, f32[128,16]{0,1:T(8,128)S(1)}, u32[]{:S(2)}, u32[]{:S(2)}) collective-permute-start(f32[128,16]{0,1:T(8,128)} %bitcast_reduce_fusion), channel_id=1, source_target_pairs={{0,16},{1,17},{2,18},{3,19},{4,20},{5,21},{6,22},{7,23},{8,24},{9,... | collective-permute-start | bytes 24584 | tf_op jit(solution)/shard_map/ppermute | solution.py:24
  75.3 71.9 %collective-permute-start.15 = (f32[128,16]{0,1:T(8,128)}, f32[128,16]{0,1:T(8,128)S(1)}, u32[]{:S(2)}, u32[]{:S(2)}) collective-permute-start(f32[128,16]{0,1:T(8,128)} %bitcast_reduce_fusion), channel_id=1, source_target_pairs={{16,0},{17,1},{18,2},{19,3},{20,4},{21,5},{22,6},{23,7},{24,8},{25... | collective-permute-start | bytes 24584 | tf_op jit(solution)/shard_map/ppermute | solution.py:24
  76.6 71.3 %collective-permute-start.12 = (bf16[128,1024]{1,0:T(8,128)(2,1)}, bf16[128,1024]{1,0:T(8,128)(2,1)}, u32[]{:S(2)}, u32[]{:S(2)}) collective-permute-start(bf16[128,1024]{1,0:T(8,128)(2,1)} %get-tuple-element.396), channel_id=1, source_target_pairs={{0,16},{1,17},{2,18},{3,19},{4,20},{5,21},{6,22},{7,23},{8,24},{9,... | collective-permute-start | bytes 786440 | tf_op jit(solution)/shard_map/ppermute | solution.py:24
  81.8 66.0 %collective-permute-start.13 = (bf16[128,1024]{1,0:T(8,128)(2,1)}, bf16[128,1024]{1,0:T(8,128)(2,1)}, u32[]{:S(2)}, u32[]{:S(2)}) collective-permute-start(bf16[128,1024]{1,0:T(8,128)(2,1)} %get-tuple-element.396), channel_id=1, source_target_pairs={{16,0},{17,1},{18,2},{19,3},{20,4},{21,5},{22,6},{23,7},{24,8},{25... | collective-permute-start | bytes 786440 | tf_op jit(solution)/shard_map/ppermute | solution.py:24
  84.9 15.8 %copy-start.1 = (bf16[1024,1024]{1,0:T(8,128)(2,1)S(1)}, bf16[1024,1024]{1,0:T(8,128)(2,1)}, u32[]{:S(2)}) copy-start(bf16[1024,1024]{1,0:T(8,128)(2,1)} %all-gather.2.cloned.1.call-done) | copy-start | bytes 6291460
  147.9 1.7 copy-start.4
  147.9 1.7 copy-start.5
Sparse Core Ops, SparseCore 0:
  22.6 43.8 all-gather.1
  70.4 71.6 reduce-scatter.1
  149.7 19.4 all-reduce.1
